TPU v7x, 32 devices: a whole 2x2x4 slice. The times are simulated.
32 devices in a mesh: grp: 2 (over y), kvp: 4 (over x, core), tp: 4 (over z).
Axes of the slice: x: 2, y: 2, z: 4, core: 2. Of those that a mesh axis runs over, the one named last changes fastest.
Arguments:
- hidden_in: bfloat16 [16, 7168], P('grp'), parts along dimension 0, may hold values from -3 to 3
- queries_nope: bfloat16 [16, 128, 128], P('grp', ('kvp', 'tp')), parts along dimension 0, may hold values from -6 to 6
- queries_rope: bfloat16 [16, 128, 64], P('grp', ('kvp', 'tp')), parts along dimension 0, may hold values from -26 to 26
- cache: bfloat16 [16, 1536, 576], P('grp', 'kvp'), parts along dimension 0, may hold values from -20 to 20
- lengths: int32 [16], P('grp'), parts along dimension 0, may hold values from 128 to 1536, as said below
- w_uk: bfloat16 [128, 128, 512], P(('kvp', 'tp')), may hold values from -0.5 to 0.5
- w_uv: bfloat16 [128, 512, 128], P(('kvp', 'tp')), may hold values from -0.25 to 0.25
- w_out: bfloat16 [16384, 7168], P(('kvp', 'tp')), may hold values from -0.0625 to 0.0625
- norm_gain: float32 [7168], replicated, may hold values from 0.25 to 1.75
- w_gate: bfloat16 [7168, 18432], P(None, ('kvp', 'tp')), may hold values from -0.0625 to 0.0625
- w_up: bfloat16 [7168, 18432], P(None, ('kvp', 'tp')), may hold values from -0.0625 to 0.0625
- w_down: bfloat16 [18432, 7168], P(('kvp', 'tp')), may hold values from -0.0625 to 0.0625
Outputs:
- layer_out: bfloat16 [16, 7168], P('grp', ('kvp', 'tp')), parts along dimension 0
There are 2 independent parts, one for each index of `grp`. A program takes and returns all parts, laid end to end along the dimension named above; an argument that names none is the same for every part. Nothing has to cross between parts.
Inputs may be any that keep to these rules, and one draw needn't show every extreme that they name: `lengths`: every length is a multiple of 128; in every draw some request has the full 1536.
All inputs are finite; a program needn't handle non-finite values.
Results may differ from a plain program's by a relative error of at most 0.04.
Values may be sent and summed in bfloat16 or wider, within the bound.
A program may use at most 128 MiB of HBM per device.

v0:
```python
import jax
import jax.numpy as jnp
from jax import lax
from jax.sharding import PartitionSpec as P


def project(o_lat, w_uv, w_out):
    head_out = jnp.einsum("bhl,hle->bhe", o_lat, w_uv, preferred_element_type=jnp.float32).astype(
        jnp.bfloat16
    )
    return jnp.dot(
        head_out.reshape(head_out.shape[0], -1), w_out, preferred_element_type=jnp.float32
    )


def per_device(
    hidden_in,
    queries_nope,
    queries_rope,
    cache,
    lengths,
    w_uk,
    w_uv,
    w_out,
    norm_gain,
    w_gate,
    w_up,
    w_down,
):
    batch, heads_dev, head_dim = queries_nope.shape
    latent = w_uk.shape[2]
    ctx_dev = cache.shape[1]
    groups = lax.axis_size("kvp")
    score_scale = float(head_dim + queries_rope.shape[2]) ** (-0.5)
    q_lat = jnp.einsum(
        "bhd,hdl->bhl", queries_nope, w_uk, preferred_element_type=jnp.float32
    ).astype(jnp.bfloat16)
    q_lat_all, rope_all = (
        lax.all_gather(q_lat, "kvp", axis=1, tiled=True),
        lax.all_gather(queries_rope, "kvp", axis=1, tiled=True),
    )
    q_full = jnp.concatenate([q_lat_all, rope_all], axis=2)
    scores = (
        jnp.einsum("bhc,btc->bht", q_full, cache, preferred_element_type=jnp.float32) * score_scale
    )
    offset = lax.axis_index("kvp") * ctx_dev
    visible = ((offset + jnp.arange(ctx_dev, dtype=jnp.int32))[None, :] < lengths[:, None])[
        :, None, :
    ]
    masked = jnp.where(visible, scores, jnp.float32(-1e30))
    block_max = jnp.max(masked, axis=2)
    exponent = jnp.where(visible, jnp.exp(masked - block_max[..., None]), jnp.float32(0.0))
    guarded = jnp.maximum(jnp.sum(exponent, axis=2), 1.0)
    log_total = block_max + jnp.log(guarded)
    weights = (exponent / guarded[..., None]).astype(jnp.bfloat16)
    partial_value = jnp.einsum("bht,btc->bhc", weights, cache, preferred_element_type=jnp.float32)[
        ..., :latent
    ]
    blocks = partial_value.reshape(batch, groups, heads_dev, latent)
    block_logs = log_total.reshape(batch, groups, heads_dev)
    part_blocks = lax.all_to_all(
        blocks.astype(jnp.bfloat16), "kvp", split_axis=1, concat_axis=1, tiled=True
    ).astype(blocks.dtype)
    part_logs = lax.all_to_all(
        block_logs.astype(jnp.bfloat16), "kvp", split_axis=1, concat_axis=1, tiled=True
    ).astype(block_logs.dtype)
    highest = jnp.max(part_logs, axis=1)
    overall = highest + jnp.log(jnp.sum(jnp.exp(part_logs - highest[:, None, :]), axis=1))
    scaled = jnp.exp(part_logs - overall[:, None, :])[..., None] * part_blocks
    o_lat = jnp.sum(scaled, axis=1).astype(jnp.bfloat16)
    attention = project(o_lat, w_uv, w_out)
    model_width = norm_gain.shape[0]
    share_width = model_width // lax.axis_size(("kvp", "tp"))
    share_start = lax.axis_index(("kvp", "tp")) * share_width
    attn_whole = lax.psum(attention, ("kvp", "tp"))
    residual = hidden_in.astype(jnp.float32) + attn_whole
    mean_square = jnp.mean(residual * residual, axis=1)
    normed = (residual * lax.rsqrt(mean_square + 1e-06)[:, None] * norm_gain[None, :]).astype(
        jnp.bfloat16
    )
    residual_share = lax.dynamic_slice_in_dim(residual, share_start, share_width, 1)
    gate_proj = jnp.dot(normed, w_gate, preferred_element_type=jnp.float32)
    up_proj = jnp.dot(normed, w_up, preferred_element_type=jnp.float32)
    act = (jax.nn.silu(gate_proj) * up_proj).astype(jnp.bfloat16)
    ffn_terms = jnp.dot(act, w_down, preferred_element_type=jnp.float32)
    ffn_share = lax.psum_scatter(ffn_terms, ("kvp", "tp"), scatter_dimension=1, tiled=True)
    return (residual_share + ffn_share).astype(jnp.bfloat16)


def solution(mesh):
    placed = (
        P("grp", None),
        P("grp", ("kvp", "tp"), None),
        P("grp", ("kvp", "tp"), None),
        P("grp", "kvp", None),
        P("grp"),
        P(("kvp", "tp"), None, None),
        P(("kvp", "tp"), None, None),
        P(("kvp", "tp"), None),
        P(),
        P(None, ("kvp", "tp")),
        P(None, ("kvp", "tp")),
        P(("kvp", "tp"), None),
    )
    return jax.shard_map(
        per_device, mesh=mesh, in_specs=placed, out_specs=P("grp", ("kvp", "tp")), check_vma=False
    )
```

profile of v0, /device:TPU:0, one launch (start us, length us, event | category | flops | bytes accessed | tf_op | source)
XLA Modules:
  0.0 248.7 jit_solution(1045707272200250479)
XLA Ops:
  6.5 0.0 copy-start
  6.5 0.9 copy.24
  7.4 6.3 %all_gather.7 = bf16[8,32,64]{2,0,1:T(8,128)(2,1)S(1)} all-gather(bf16[8,8,64]{2,0,1:T(8,128)(2,1)S(1)} %copy.24), channel_id=1, replica_groups=mesh['grp'=2,'kvp'=4,'tp'=4] {'kvp'}, dimensions={1}, use_global_device_ids=true | all-gather | bytes 40960 | tf_op jit(solution)/shard_map/all_gather | solution.py:40
  13.7 1.5 fusion.2
  15.2 6.3 %all_gather.6 = bf16[8,32,512]{2,0,1:T(8,128)(2,1)S(1)} all-gather(bf16[8,8,512]{2,0,1:T(8,128)(2,1)S(1)} %fusion.2), channel_id=1, replica_groups=mesh['grp'=2,'kvp'=4,'tp'=4] {'kvp'}, dimensions={1}, use_global_device_ids=true | all-gather | bytes 327680 | tf_op jit(solution)/shard_map/all_gather | solution.py:39
  21.5 0.1 copy.25
  21.6 0.7 broadcast_compare_fusion
  22.3 0.0 copy-done
  22.3 0.7 fusion.31
  23.0 0.0 copy-start.3
  23.0 0.7 copy-done.3
  23.8 0.2 fusion.8
  24.0 0.6 add_convert_fusion.1
  24.6 0.8 convert_element_type.50
  25.3 0.6 copy.27
  25.9 3.2 %all-to-all-start = ((bf16[8,4,8]{2,0,1:T(8,128)(2,1)}), bf16[8,4,8]{2,0,1:T(8,128)(2,1)S(1)}, u32[]{:S(2)}, u32[]{:S(2)}) async-start(bf16[8,4,8]{2,0,1:T(8,128)(2,1)} %copy.27), calls=%async_computation | async-start | bytes 16384 | tf_op jit(solution)/shard_map/all_to_all | solution.py:64
  29.2 2.2 fusion.10
  31.4 0.0 copy-start.5
  31.5 0.0 copy-start.4
  31.5 0.7 copy.28
  32.2 0.8 all-to-all-done
  33.0 3.4 %all-to-all-start.1 = ((bf16[8,4,8,512]{3,2,0,1:T(8,128)(2,1)}), bf16[8,4,8,512]{3,2,0,1:T(8,128)(2,1)S(1)}, u32[]{:S(2)}, u32[]{:S(2)}) async-start(bf16[8,4,8,512]{3,2,0,1:T(8,128)(2,1)} %copy.28), calls=%async_computation.1 | async-start | bytes 524288 | tf_op jit(solution)/shard_map/all_to_all | solution.py:61
  36.4 0.0 all-reduce.2.cloned.1.call-start
  36.5 5.8 %all-to-all-done.1 = bf16[8,4,8,512]{3,2,0,1:T(8,128)(2,1)S(1)} async-done(((bf16[8,4,8,512]{3,2,0,1:T(8,128)(2,1)}), bf16[8,4,8,512]{3,2,0,1:T(8,128)(2,1)S(1)}, u32[]{:S(2)}, u32[]{:S(2)}) %all-to-all-start.1) | async-done | bytes 262176 | tf_op jit(solution)/shard_map/all_to_all | solution.py:61
  42.4 0.1 multiply_reduce_fusion
  42.5 8.4 %fusion.4 = f32[8,7168]{1,0:T(8,128)} fusion(bf16[1024,7168]{1,0:T(8,128)(2,1)} %param.19, bf16[8,512,128]{2,1,0:T(8,128)(2,1)} %param.18, bf16[8,8,512]{2,1,0:T(8,128)(2,1)S(1)} %multiply_reduce_fusion), kind=kOutput, calls=%fused_computation.9 | convolution fusion | flops 125837312 | bytes 16023552 | tf_op jit(solution)/shard_map/dot_general | solution.py:11
  50.8 0.0 all-reduce.2.cloned.1.call-update
  50.9 0.0 reduce-scatter.4.cloned.1.call-start
  50.9 89.8 %all-reduce.2.cloned.1.call-done = f32[8,7168]{1,0:T(8,128)} async-done(((f32[8,7168]{1,0:T(8,128)}), f32[8,7168]{1,0:T(8,128)}) %all-reduce.2.cloned.1.call-update) | async-done | bytes 229392 | tf_op jit(solution)/shard_map/psum | solution.py:75
  140.7 0.0 copy-done.5
  140.7 1.1 multiply_reduce_fusion.1
  141.8 0.0 copy-start.2
  141.8 0.7 copy-done.2
  142.5 0.0 copy-done.4
  142.5 8.6 %fusion.30 = f32[8,1152]{1,0:T(8,128)} fusion(bf16[7168,1152]{1,0:T(8,128)(2,1)} %param.21, f32[8,7168]{1,0:T(8,128)S(1)} %get-tuple-element.6, f32[7168]{0:T(1024)S(1)} %copy-done.4, f32[8]{0:T(128)S(1)} %add_rsqrt_fusion), kind=kOutput, calls=%fused_computation.50 | convolution fusion | flops 132292608 | bytes 16810016 | tf_op jit(solution)/shard_map/dot_general | solution.py:82
  151.1 0.0 copy-start.1
  151.1 18.6 %convolution_bitcast_fusion = f32[7168,8]{1,0:T(8,128)} fusion(bf16[1152,7168]{1,0:T(8,128)(2,1)} %param.23, bf16[7168,1152]{1,0:T(8,128)(2,1)} %param.22, f32[8,1152]{1,0:T(8,128)} %fusion.30, f32[8,7168]{1,0:T(8,128)} %copy-done.2, f32[7168]{0:T(1024)} %param.20, f32[8]{0:T(128)S(1)} %add_rsqrt_fusion), kind=kOutput, calls=%fused_computation | convolution fusion | flops 264468480 | bytes 33554464
  169.7 0.0 reduce-scatter.4.cloned.1.call-update
  169.7 69.7 %reduce-scatter.4.cloned.1.call-done = f32[448,8]{1,0:T(8,128)} async-done(((f32[7168,8]{1,0:T(8,128)}), f32[448,8]{1,0:T(8,128)}) %reduce-scatter.4.cloned.1.call-update) | async-done | bytes 14352
  239.4 1.0 copy.32
  240.4 1.4 add_convert_fusion
  241.9 0.0 copy-done.1
  (9 shorter events, 0.1 us)
Async XLA Ops:
  6.5 15.7 %copy-start = (bf16[8,384,576]{1,2,0:T(8,128)(2,1)S(1)}, bf16[8,384,576]{1,2,0:T(8,128)(2,1)}, u32[]{:S(2)}) copy-start(bf16[8,384,576]{1,2,0:T(8,128)(2,1)} %param.15) | copy-start | bytes 10616836
  23.0 0.7 copy-start.3
  25.9 7.0 %all-to-all-start = ((bf16[8,4,8]{2,0,1:T(8,128)(2,1)}), bf16[8,4,8]{2,0,1:T(8,128)(2,1)S(1)}, u32[]{:S(2)}, u32[]{:S(2)}) async-start(bf16[8,4,8]{2,0,1:T(8,128)(2,1)} %copy.27), calls=%async_computation | async-start | bytes 16384 | tf_op jit(solution)/shard_map/all_to_all | solution.py:64
  31.4 109.2 %copy-start.5 = (bf16[8,7168]{1,0:T(8,128)(2,1)S(1)}, bf16[8,7168]{1,0:T(8,128)(2,1)}, u32[]{:S(2)}) copy-start(bf16[8,7168]{1,0:T(8,128)(2,1)} %param.12) | copy-start | bytes 344068
  31.5 111.0 %copy-start.4 = (f32[7168]{0:T(1024)S(1)}, f32[7168]{0:T(1024)}, u32[]{:S(2)}) copy-start(f32[7168]{0:T(1024)} %param.20) | copy-start | bytes 86020
  33.0 9.4 %all-to-all-start.1 = ((bf16[8,4,8,512]{3,2,0,1:T(8,128)(2,1)}), bf16[8,4,8,512]{3,2,0,1:T(8,128)(2,1)S(1)}, u32[]{:S(2)}, u32[]{:S(2)}) async-start(bf16[8,4,8,512]{3,2,0,1:T(8,128)(2,1)} %copy.28), calls=%async_computation.1 | async-start | bytes 524288 | tf_op jit(solution)/shard_map/all_to_all | solution.py:61
  36.4 104.3 %all-reduce.2.cloned.1.call-start = ((), (), s32[]{:S(2)}) async-start(), calls=%async_computation.3 | async-start | bytes 458752 | tf_op jit(solution)/shard_map/psum | solution.py:75
  50.9 188.6 %reduce-scatter.4.cloned.1.call-start = ((), (), s32[]{:S(2)}) async-start(), calls=%async_computation.4 | async-start | bytes 3899392
  141.8 0.7 copy-start.2
  151.1 90.8 %copy-start.1 = (bf16[8,384,576]{1,2,0:T(8,128)(2,1)S(1)}, bf16[8,384,576]{1,2,0:T(8,128)(2,1)}, u32[]{:S(2)}) copy-start(bf16[8,384,576]{1,2,0:T(8,128)(2,1)} %param.15) | copy-start | bytes 10616836
Sparse Core Ops, SparseCore 0:
  51.0 89.6 all-reduce.1
  169.9 69.5 reduce-scatter.3
where the time goes:
time: 249 us
  waiting for transfers between devices  166 us (67%)
  matrix products  40 us (16%)
  between operations  13.5 us (5%)
  blocking collectives  12.6 us (5%)
  starting transfers between devices  6.74 us (3%)
  local copies, waits for them, and re-layouts  5.54 us (2%)
  other arithmetic  4.23 us (2%)
    psum x1, waiting for transfers between devices, per_device(): attn_whole = lax.psum(attention, ('kvp', 'tp'))  89.8 us
    unnamed x3, waiting for transfers between devices  69.7 us
    unnamed x1, matrix products  18.6 us
    dot_general x1, matrix products, per_device(): gate_proj = jnp.dot(normed, w_gate, preferred_element_type=jnp.float32)  8.58 us
    dot_general x1, matrix products, project(): jnp.dot(head_out.reshape(head_out.shape[0], -1), w_out, preferred_element...  8.36 us
    all_gather x1, blocking collectives, per_device(): lax.all_gather(queries_rope, 'kvp', axis=1, tiled=True)  6.3 us
    all_gather x1, blocking collectives, per_device(): lax.all_gather(q_lat, 'kvp', axis=1, tiled=True)  6.27 us
    all_to_all x1, waiting for transfers between devices, per_device(): lax.all_to_all(blocks.astype(jnp.bfloat16), 'kvp', split_axis=1, concat_a...  5.84 us
  transfers between devices with their start and end apart: 4, of which 4 were waited for; matrix products, arithmetic and copies ran while one was open for 1% of the time, Pallas kernels for 0%

commit v1 on v0

--- a/solution.py
+++ b/solution.py
@@ -72,7 +72,7 @@
     model_width = norm_gain.shape[0]
     share_width = model_width // lax.axis_size(("kvp", "tp"))
     share_start = lax.axis_index(("kvp", "tp")) * share_width
-    attn_whole = lax.psum(attention, ("kvp", "tp"))
+    attn_whole = lax.psum(lax.psum(attention, "tp"), "kvp")
     residual = hidden_in.astype(jnp.float32) + attn_whole
     mean_square = jnp.mean(residual * residual, axis=1)
     normed = (residual * lax.rsqrt(mean_square + 1e-06)[:, None] * norm_gain[None, :]).astype(

time: 249 us -> 228 us (0.916)
  waiting for transfers between devices: 166 us -> 145 us
    psum x1 -> x2, waiting for transfers between devices: 89.8 us -> 69.9 us  [per_device(): attn_whole = lax.psum(lax.psum(attention, 'tp'), 'kvp')]
    unnamed x3 -> x4, waiting for transfers between devices: 69.7 us -> 68.8 us
  transfers between devices with their start and end apart: 4 -> 5, of which waited for: 4 -> 5; matrix products, arithmetic and copies ran while one was open for 1% -> 1% of each run, Pallas kernels for 0% -> 0%
where the time goes in v1:
time: 228 us
  waiting for transfers between devices  145 us (64%)
  matrix products  40 us (18%)
  between operations  13.2 us (6%)
  blocking collectives  12.6 us (6%)
  starting transfers between devices  6.78 us (3%)
  local copies, waits for them, and re-layouts  5.54 us (2%)
  other arithmetic  4.23 us (2%)
    psum x2, waiting for transfers between devices, per_device(): attn_whole = lax.psum(lax.psum(attention, 'tp'), 'kvp')  69.9 us
    unnamed x4, waiting for transfers between devices  68.8 us
    unnamed x1, matrix products  18.6 us
    dot_general x1, matrix products, per_device(): gate_proj = jnp.dot(normed, w_gate, preferred_element_type=jnp.float32)  8.58 us
    dot_general x1, matrix products, project(): jnp.dot(head_out.reshape(head_out.shape[0], -1), w_out, preferred_element...  8.36 us
    all_gather x1, blocking collectives, per_device(): lax.all_gather(queries_rope, 'kvp', axis=1, tiled=True)  6.3 us
    all_gather x1, blocking collectives, per_device(): lax.all_gather(q_lat, 'kvp', axis=1, tiled=True)  6.27 us
    all_to_all x1, waiting for transfers between devices, per_device(): lax.all_to_all(blocks.astype(jnp.bfloat16), 'kvp', split_axis=1, concat_a...  5.84 us
  transfers between devices with their start and end apart: 5, of which 5 were waited for; matrix products, arithmetic and copies ran while one was open for 1% of the time, Pallas kernels for 0%

profile of v1, /device:TPU:0, one launch (start us, length us, event | category | flops | bytes accessed | tf_op | source)
XLA Modules:
  0.0 227.6 jit_solution(4861955756876073280)
XLA Ops:
  6.5 0.0 copy-start
  6.5 0.9 copy.24
  7.4 6.3 %all_gather.7 = bf16[8,32,64]{2,0,1:T(8,128)(2,1)S(1)} all-gather(bf16[8,8,64]{2,0,1:T(8,128)(2,1)S(1)} %copy.24), channel_id=1, replica_groups=mesh['grp'=2,'kvp'=4,'tp'=4] {'kvp'}, dimensions={1}, use_global_device_ids=true | all-gather | bytes 40960 | tf_op jit(solution)/shard_map/all_gather | solution.py:40
  13.7 1.5 fusion.2
  15.2 6.3 %all_gather.6 = bf16[8,32,512]{2,0,1:T(8,128)(2,1)S(1)} all-gather(bf16[8,8,512]{2,0,1:T(8,128)(2,1)S(1)} %fusion.2), channel_id=1, replica_groups=mesh['grp'=2,'kvp'=4,'tp'=4] {'kvp'}, dimensions={1}, use_global_device_ids=true | all-gather | bytes 327680 | tf_op jit(solution)/shard_map/all_gather | solution.py:39
  21.5 0.1 copy.25
  21.6 0.7 broadcast_compare_fusion
  22.3 0.0 copy-done
  22.3 0.7 fusion.31
  23.0 0.0 copy-start.3
  23.0 0.7 copy-done.3
  23.8 0.2 fusion.8
  24.0 0.6 add_convert_fusion.1
  24.6 0.8 convert_element_type.50
  25.3 0.6 copy.27
  25.9 3.2 %all-to-all-start = ((bf16[8,4,8]{2,0,1:T(8,128)(2,1)}), bf16[8,4,8]{2,0,1:T(8,128)(2,1)S(1)}, u32[]{:S(2)}, u32[]{:S(2)}) async-start(bf16[8,4,8]{2,0,1:T(8,128)(2,1)} %copy.27), calls=%async_computation | async-start | bytes 16384 | tf_op jit(solution)/shard_map/all_to_all | solution.py:64
  29.2 2.2 fusion.10
  31.4 0.0 copy-start.5
  31.5 0.0 copy-start.4
  31.5 0.7 copy.28
  32.2 0.8 all-to-all-done
  33.0 3.4 %all-to-all-start.1 = ((bf16[8,4,8,512]{3,2,0,1:T(8,128)(2,1)}), bf16[8,4,8,512]{3,2,0,1:T(8,128)(2,1)S(1)}, u32[]{:S(2)}, u32[]{:S(2)}) async-start(bf16[8,4,8,512]{3,2,0,1:T(8,128)(2,1)} %copy.28), calls=%async_computation.1 | async-start | bytes 524288 | tf_op jit(solution)/shard_map/all_to_all | solution.py:61
  36.4 0.0 all-reduce.3.cloned.1.call-start
  36.5 5.8 %all-to-all-done.1 = bf16[8,4,8,512]{3,2,0,1:T(8,128)(2,1)S(1)} async-done(((bf16[8,4,8,512]{3,2,0,1:T(8,128)(2,1)}), bf16[8,4,8,512]{3,2,0,1:T(8,128)(2,1)S(1)}, u32[]{:S(2)}, u32[]{:S(2)}) %all-to-all-start.1) | async-done | bytes 262176 | tf_op jit(solution)/shard_map/all_to_all | solution.py:61
  42.4 0.1 multiply_reduce_fusion
  42.5 8.4 %fusion.4 = f32[8,7168]{1,0:T(8,128)} fusion(bf16[1024,7168]{1,0:T(8,128)(2,1)} %param.19, bf16[8,512,128]{2,1,0:T(8,128)(2,1)} %param.18, bf16[8,8,512]{2,1,0:T(8,128)(2,1)S(1)} %multiply_reduce_fusion), kind=kOutput, calls=%fused_computation.9 | convolution fusion | flops 125837312 | bytes 16023552 | tf_op jit(solution)/shard_map/dot_general | solution.py:11
  50.8 0.0 all-reduce.3.cloned.1.call-update
  50.9 0.0 all-reduce.5.cloned.1.call-start
  50.9 35.7 %all-reduce.3.cloned.1.call-done = f32[8,7168]{1,0:T(8,128)} async-done(((f32[8,7168]{1,0:T(8,128)}), f32[8,7168]{1,0:T(8,128)}) %all-reduce.3.cloned.1.call-update) | async-done | bytes 229392 | tf_op jit(solution)/shard_map/psum | solution.py:75
  86.6 0.0 all-reduce.5.cloned.1.call-update
  86.6 0.0 reduce-scatter.4.cloned.1.call-start
  86.6 34.2 %all-reduce.5.cloned.1.call-done = f32[8,7168]{1,0:T(8,128)} async-done(((f32[8,7168]{1,0:T(8,128)}), f32[8,7168]{1,0:T(8,128)}) %all-reduce.5.cloned.1.call-update) | async-done | bytes 229392 | tf_op jit(solution)/shard_map/psum | solution.py:75
  120.9 0.0 copy-done.5
  120.9 1.1 multiply_reduce_fusion.1
  122.0 0.0 copy-start.2
  122.0 0.7 copy-done.2
  122.7 0.0 copy-done.4
  122.7 8.6 %fusion.30 = f32[8,1152]{1,0:T(8,128)} fusion(bf16[7168,1152]{1,0:T(8,128)(2,1)} %param.21, f32[8,7168]{1,0:T(8,128)S(1)} %get-tuple-element.6, f32[7168]{0:T(1024)S(1)} %copy-done.4, f32[8]{0:T(128)S(1)} %add_rsqrt_fusion), kind=kOutput, calls=%fused_computation.50 | convolution fusion | flops 132292608 | bytes 16810016 | tf_op jit(solution)/shard_map/dot_general | solution.py:82
  131.2 0.0 copy-start.1
  131.2 18.6 %convolution_bitcast_fusion = f32[7168,8]{1,0:T(8,128)} fusion(bf16[1152,7168]{1,0:T(8,128)(2,1)} %param.23, bf16[7168,1152]{1,0:T(8,128)(2,1)} %param.22, f32[8,1152]{1,0:T(8,128)} %fusion.30, f32[8,7168]{1,0:T(8,128)} %copy-done.2, f32[7168]{0:T(1024)} %param.20, f32[8]{0:T(128)S(1)} %add_rsqrt_fusion), kind=kOutput, calls=%fused_computation | convolution fusion | flops 264468480 | bytes 33554464
  149.9 0.0 reduce-scatter.4.cloned.1.call-update
  149.9 68.7 %reduce-scatter.4.cloned.1.call-done = f32[448,8]{1,0:T(8,128)} async-done(((f32[7168,8]{1,0:T(8,128)}), f32[448,8]{1,0:T(8,128)}) %reduce-scatter.4.cloned.1.call-update) | async-done | bytes 14352
  218.6 1.0 copy.32
  219.7 1.4 add_convert_fusion
  221.1 0.0 copy-done.1
  (9 shorter events, 0.1 us)
Async XLA Ops:
  6.5 15.7 %copy-start = (bf16[8,384,576]{1,2,0:T(8,128)(2,1)S(1)}, bf16[8,384,576]{1,2,0:T(8,128)(2,1)}, u32[]{:S(2)}) copy-start(bf16[8,384,576]{1,2,0:T(8,128)(2,1)} %param.15) | copy-start | bytes 10616836
  23.0 0.7 copy-start.3
  25.9 7.0 %all-to-all-start = ((bf16[8,4,8]{2,0,1:T(8,128)(2,1)}), bf16[8,4,8]{2,0,1:T(8,128)(2,1)S(1)}, u32[]{:S(2)}, u32[]{:S(2)}) async-start(bf16[8,4,8]{2,0,1:T(8,128)(2,1)} %copy.27), calls=%async_computation | async-start | bytes 16384 | tf_op jit(solution)/shard_map/all_to_all | solution.py:64
  31.4 89.4 %copy-start.5 = (bf16[8,7168]{1,0:T(8,128)(2,1)S(1)}, bf16[8,7168]{1,0:T(8,128)(2,1)}, u32[]{:S(2)}) copy-start(bf16[8,7168]{1,0:T(8,128)(2,1)} %param.12) | copy-start | bytes 344068
  31.5 91.2 %copy-start.4 = (f32[7168]{0:T(1024)S(1)}, f32[7168]{0:T(1024)}, u32[]{:S(2)}) copy-start(f32[7168]{0:T(1024)} %param.20) | copy-start | bytes 86020
  33.0 9.4 %all-to-all-start.1 = ((bf16[8,4,8,512]{3,2,0,1:T(8,128)(2,1)}), bf16[8,4,8,512]{3,2,0,1:T(8,128)(2,1)S(1)}, u32[]{:S(2)}, u32[]{:S(2)}) async-start(bf16[8,4,8,512]{3,2,0,1:T(8,128)(2,1)} %copy.28), calls=%async_computation.1 | async-start | bytes 524288 | tf_op jit(solution)/shard_map/all_to_all | solution.py:61
  36.4 50.2 %all-reduce.3.cloned.1.call-start = ((), (), s32[]{:S(2)}) async-start(), calls=%async_computation.3 | async-start | bytes 458752 | tf_op jit(solution)/shard_map/psum | solution.py:75
  50.9 70.0 %all-reduce.5.cloned.1.call-start = ((), (), s32[]{:S(2)}) async-start(), calls=%async_computation.4 | async-start | bytes 458752 | tf_op jit(solution)/shard_map/psum | solution.py:75
  86.6 132.0 %reduce-scatter.4.cloned.1.call-start = ((), (), s32[]{:S(2)}) async-start(), calls=%async_computation.5 | async-start | bytes 3899392
  122.0 0.7 copy-start.2
  131.2 89.8 %copy-start.1 = (bf16[8,384,576]{1,2,0:T(8,128)(2,1)S(1)}, bf16[8,384,576]{1,2,0:T(8,128)(2,1)}, u32[]{:S(2)}) copy-start(bf16[8,384,576]{1,2,0:T(8,128)(2,1)} %param.15) | copy-start | bytes 10616836
Sparse Core Ops, SparseCore 0:
  51.0 35.5 all-reduce.2
  88.9 31.9 all-reduce.4
  150.0 68.5 reduce-scatter.3
